TPU v7x, 32 devices: a whole 2x2x4 slice. The times are simulated.
32 devices in a mesh: chan: 8 (over z, y), bins: 4 (over x, core).
Axes of the slice: x: 2, y: 2, z: 4, core: 2. Of those that a mesh axis runs over, the one named last changes fastest.
Arguments:
- effects: bfloat16 [64, 8192, 256], P('chan', 'bins'), may hold values from -0.19921875 to 0.19921875
- nominal: float32 [64, 8192], P('chan', 'bins'), may hold values from 0.2 to 5
- observed: int32 [64, 8192], P('chan', 'bins'), may hold values from 0 to 7
- mc_variance: float32 [64, 8192], P('chan', 'bins'), may hold values from 0.002 to 0.5
- theta: float32 [8192], replicated, may hold values from -4 to 4
- nuisance_index: int32 [64, 256], replicated, may hold values from 0 to 8191, as said below
- bin_counts: int32 [64], P('chan'), may hold values from 1 to 8192, 262144 in all
- tile_owner: int32 [256], replicated, may hold values from 0 to 255, each once
Outputs:
- hessian_tiles: float32 [256, 512, 512], P(('chan', 'bins'))
- gradient: float32 [8192], P(('chan', 'bins'))
Inputs may be any that keep to these rules, and one draw needn't show every extreme that they name: `nuisance_index`: each channel's list is 2 runs of 128 consecutive nuisances, each run starting at a multiple of 128, the runs distinct and in increasing order. Bins at positions bin_counts[c] and beyond of channel c carry no data. `tile_owner`: every tile number appears exactly once.
All inputs are finite; a program needn't handle non-finite values. No bound on the sum of `bin_counts` on one device may be relied on, other than what follows from the above.
Results may differ from a plain program's by a relative error of at most 0.0029.
Values sent between devices are 32-bit elements; how exact they have to be, the bound alone decides.
A program may use at most 128 MiB of HBM per device.

v0:
```python
import jax
import jax.numpy as jnp
from jax import lax
from jax.sharding import PartitionSpec as P

GW = 128
TILE = 512


def group_vector(values, groups, group_count):
    choose = (groups[:, :, None] == jnp.arange(group_count, dtype=jnp.int32)[None, None, :]).astype(
        jnp.float32
    )
    return jnp.einsum("nrg,nrw->gw", choose, values, precision=lax.Precision.HIGHEST).reshape(-1)


def place_blocks(blocks, groups, slot_lookup, group_start, slot_count, per_tile, tile_side):
    chans_total, group_parts, run_width = (blocks.shape[0], blocks.shape[1], blocks.shape[2])
    sub_blocks = jnp.transpose(blocks, (0, 1, 3, 2, 4)).reshape(
        chans_total * group_parts * group_parts, run_width, run_width
    )
    row_group = jnp.broadcast_to(groups[:, :, None], (chans_total, group_parts, group_parts))
    col_group = jnp.broadcast_to(groups[:, None, :], (chans_total, group_parts, group_parts))
    tile_ids = row_group // per_tile * tile_side + col_group // per_tile
    slot_ids = slot_lookup[tile_ids] - group_start
    inside = jnp.logical_and(slot_ids >= 0, slot_ids < slot_count)
    slot_ids = jnp.where(inside, slot_ids, slot_count).reshape(-1)
    row_offset = (row_group % per_tile).reshape(-1)
    col_offset = (col_group % per_tile).reshape(-1)
    placed_buffer = jnp.zeros((slot_count, per_tile, per_tile, run_width, run_width), jnp.float32)
    placed_buffer = placed_buffer.at[slot_ids, row_offset, col_offset].add(sub_blocks, mode="drop")
    side_len = per_tile * run_width
    return jnp.transpose(placed_buffer, (0, 1, 3, 2, 4)).reshape(slot_count, side_len, side_len)


def local(effects, nominal, observed, mc_variance, theta, nuisance_index, bin_counts, tile_owner):
    chan_size = lax.axis_size("chan")
    bins_size = lax.axis_size("bins")
    chan_index = lax.axis_index("chan")
    bins_index = lax.axis_index("bins")
    chans_local, bins_local, width = effects.shape
    total_nu = theta.shape[0]
    group_parts = width // GW
    group_count = total_nu // GW
    per_tile = TILE // GW
    tile_side = total_nu // TILE
    chans_here = chans_local // bins_size
    tile_total = tile_owner.shape[0]
    tiles_dev = tile_total // (chan_size * bins_size)
    slice_len = total_nu // (chan_size * bins_size)
    groups_all = nuisance_index[:, ::GW] // GW
    local_groups = lax.dynamic_slice_in_dim(groups_all, chan_index * chans_local, chans_local, 0)
    chosen = (
        theta.reshape(group_count, GW)[local_groups]
        .reshape(chans_local, width)
        .astype(jnp.bfloat16)
    )
    exponent = jnp.einsum("cbk,ck->cb", effects, chosen, preferred_element_type=jnp.float32)
    expected = nominal * jnp.exp(exponent)
    denominator = 1.0 + expected * mc_variance
    positions = bins_index * bins_local + lax.broadcasted_iota(
        jnp.int32, (chans_local, bins_local), 1
    )
    live = positions < bin_counts[:, None]
    residual = jnp.where(live, (expected - observed) / denominator, 0.0)
    weight = jnp.where(live, expected / denominator, 0.0)
    scaled = (jnp.sqrt(weight)[:, :, None] * effects).astype(jnp.bfloat16)
    gradient_part = jnp.einsum(
        "cbk,cb->ck", effects, residual.astype(jnp.bfloat16), preferred_element_type=jnp.float32
    )
    blocks = jnp.einsum("cbk,cbl->ckl", scaled, scaled, preferred_element_type=jnp.float32)
    mine_blocks, mine_grads = (
        lax.psum_scatter(blocks, "bins", scatter_dimension=0, tiled=True),
        lax.psum_scatter(gradient_part, "bins", scatter_dimension=0, tiled=True),
    )
    group_start = chan_index * bins_size * tiles_dev
    slot_lookup = (
        jnp.zeros((tile_total,), jnp.int32)
        .at[tile_owner]
        .set(jnp.arange(tile_total, dtype=jnp.int32))
    )
    gathered_order = jnp.arange(chan_size * chans_here, dtype=jnp.int32)
    channel_ids = (
        gathered_order // chans_here * chans_local
        + bins_index * chans_here
        + gathered_order % chans_here
    )
    gathered_groups = groups_all[channel_ids]
    every_blocks = lax.all_gather(mine_blocks, "chan", axis=0, tiled=True)
    tiles_part = place_blocks(
        every_blocks.reshape(every_blocks.shape[0], group_parts, GW, group_parts, GW),
        gathered_groups,
        slot_lookup,
        group_start,
        bins_size * tiles_dev,
        per_tile,
        tile_side,
    )
    tile_sums = lax.psum_scatter(tiles_part, "bins", scatter_dimension=0, tiled=True)
    own_ids = (
        chan_index * chans_local + bins_index * chans_here + jnp.arange(chans_here, dtype=jnp.int32)
    )
    grad_vector = group_vector(
        mine_grads.reshape(chans_here, group_parts, GW), groups_all[own_ids], group_count
    )
    grad_sum = lax.psum_scatter(grad_vector, ("chan", "bins"), scatter_dimension=0, tiled=True)
    slot_index = chan_index * bins_size + bins_index
    mine_ids = lax.dynamic_slice_in_dim(tile_owner, slot_index * tiles_dev, tiles_dev, 0)
    on_diagonal = (mine_ids // tile_side == mine_ids % tile_side).astype(jnp.float32)
    hessian_tiles = tile_sums + on_diagonal[:, None, None] * jnp.eye(TILE, dtype=jnp.float32)[None]
    gradient = grad_sum + lax.dynamic_slice_in_dim(theta, slot_index * slice_len, slice_len, 0)
    return (hessian_tiles, gradient)


def solution(mesh):
    return jax.shard_map(
        local,
        mesh=mesh,
        in_specs=(
            P("chan", "bins", None),
            P("chan", "bins"),
            P("chan", "bins"),
            P("chan", "bins"),
            P(),
            P(),
            P("chan"),
            P(),
        ),
        out_specs=(P(("chan", "bins"), None, None), P(("chan", "bins"))),
        check_vma=False,
    )
```

profile of v0, /device:TPU:0, one launch (start us, length us, event | category | flops | bytes accessed | tf_op | source)
XLA Modules:
  0.0 494.6 jit_solution(2900086767205434909)
XLA Ops:
  7.3 1.0 slice.3
  8.4 1.3 gather_fusion.2
  9.7 5.8 %fusion.25 = f32[8,1,2048]{2,1,0:T(1,128)S(1)} fusion(bf16[8,256,1]{1,2,0:T(2,128)(2,1)S(1)} %reshape.344, bf16[8,2048,256]{2,1,0:T(8,128)(2,1)} %param.8), kind=kOutput, calls=%fused_computation.86 | convolution fusion | flops 8388608 | bytes 8458240 | tf_op jit(solution)/shard_map/cbk,ck->cb/dot_general | solution.py:58
  15.5 0.1 fusion.10
  15.7 10.3 %fusion = f32[8,256,256]{2,1,0:T(8,128)} fusion(bf16[8,2048,256]{2,1,0:T(8,128)(2,1)S(1)} %copy-done, f32[8,2048]{1,0:T(8,128)S(1)} %get-tuple-element.3), kind=kOutput, calls=%fused_computation.7 | convolution fusion | flops 2160066560 | bytes 10551296 | tf_op jit(solution)/shard_map/cbk,cbl->ckl/dot_general | solution.py:71
  26.0 34.0 %reduce-scatter.3.cloned.1.call-done = f32[2,256,256]{2,1,0:T(8,128)} async-done(((f32[8,256,256]{2,1,0:T(8,128)}), f32[2,256,256]{2,1,0:T(8,128)}) %reduce-scatter.3.cloned.1.call-update) | async-done | bytes 524304 | tf_op jit(solution)/shard_map/reduce_scatter | solution.py:73
  60.2 0.6 gather_fusion
  60.8 0.1 broadcast_select_fusion.1
  60.9 0.1 select_n.201
  61.0 0.1 select_n.204
  61.1 0.1 compare_select_fusion.2
  61.2 0.1 reshape.293
  61.4 1.4 scatter_custom_fusion
  62.8 0.8 gather_fusion.1
  63.6 71.4 %all-gather.2.cloned.1.call-done = f32[16,256,256]{2,1,0:T(8,128)} async-done(((f32[2,256,256]{2,1,0:T(8,128)}), f32[16,256,256]{2,1,0:T(8,128)}) %all-gather.2.cloned.1.call-update) | async-done | bytes 4194320 | tf_op jit(solution)/shard_map/all_gather | solution.py:89
  135.0 5.7 %reshape.278 = f32[16,2,128,2,128]{4,3,2,1,0:T(2,128)} reshape(f32[16,256,256]{2,1,0:T(8,128)} %all-gather.2.cloned.1.call-done) | data formatting | bytes 8388608 | tf_op jit(solution)/shard_map/reshape | solution.py:91
  140.7 4.8 copy.19
  145.5 11.2 %broadcast_in_dim.60 = f32[32,4,4,128,128]{4,3,2,1,0:T(8,128)} broadcast(f32[]{:T(128)} %constant.127.clone.1), dimensions={} | broadcast | bytes 33554436 | tf_op jit(solution)/shard_map/broadcast_in_dim | solution.py:30
  156.8 14.2 %scatter_fusion = f32[32,4,4,128,128]{4,3,2,1,0:T(8,128)} fusion(f32[32,4,4,128,128]{4,3,2,1,0:T(8,128)} %broadcast_in_dim.60, s32[64]{0:T(128)S(1)} %fusion.24, f32[64,128,128]{2,1,0:T(8,128)} %bitcast.39), kind=kCustom, calls=%fused_computation.5 | custom fusion | flops 1048576 | bytes 12583680 | tf_op jit(solution)/shard_map/scatter-add | solution.py:31
  171.0 37.8 %copy.20 = f32[32,4,128,4,128]{4,3,2,1,0:T(4,128)} copy(f32[32,4,128,4,128]{4,2,3,1,0:T(8,128)} %bitcast.38) | data formatting | bytes 67108864 | tf_op jit(solution)/shard_map/transpose | solution.py:33
  208.8 39.2 %reshape.280 = f32[32,512,512]{2,1,0:T(8,128)} reshape(f32[32,4,128,4,128]{4,3,2,1,0:T(4,128)} %copy.20) | data formatting | bytes 67108864 | tf_op jit(solution)/shard_map/reshape | solution.py:33
  248.0 4.6 fusion.6
  252.6 0.6 dynamic-slice
  253.8 5.8 %all-reduce = f32[8,256]{1,0:T(8,128)S(1)} all-reduce(f32[8,256]{1,0:T(8,128)S(1)} %bitcast.42), channel_id=4, replica_groups=mesh['chan'=8,'bins'=4] {'bins'}, use_global_device_ids=true, to_apply=%region_4.5.clone | all-reduce | flops 2048 | bytes 16384
  259.7 0.6 gather_fusion.3
  260.2 0.3 convolution_bitcast_fusion
  260.5 39.4 %all-reduce.1 = f32[8192]{0:T(1024)S(1)} all-reduce(f32[8192]{0:T(1024)S(1)} %convolution_bitcast_fusion), channel_id=5, replica_groups=mesh['chan'=8,'bins'=4] {'chan','bins'}, use_global_device_ids=true, to_apply=%region_5.6.clone | all-reduce | flops 8192 | bytes 65536
  299.9 0.1 compare_convert_fusion
  300.0 1.3 dynamic-slice_add_fusion
  301.3 0.1 fusion.2
  301.4 178.2 %reduce-scatter.5.cloned.1.call-done = f32[8,512,512]{2,1,0:T(8,128)} async-done(((f32[32,512,512]{2,1,0:T(8,128)}), f32[8,512,512]{2,1,0:T(8,128)}) %reduce-scatter.5.cloned.1.call-update) | async-done | bytes 8388624 | tf_op jit(solution)/shard_map/reduce_scatter | solution.py:99
  479.6 8.4 %multiply_add_fusion = f32[8,512,512]{2,1,0:T(8,128)} fusion(f32[8,512,512]{2,1,0:T(8,128)} %reduce-scatter.5.cloned.1.call-done, f32[512,512]{1,0:T(8,128)S(1)} %fusion.2, f32[8]{0:T(128)S(1)} %compare_convert_fusion), kind=kLoop, calls=%fused_computation.8 | loop fusion | flops 4194304 | bytes 17825824 | tf_op jit(solution)/shard_map/add | solution.py:110
  (39 shorter events, 0.5 us)
Async XLA Ops:
  7.2 8.3 %copy-start.2 = (s32[8,2048]{1,0:T(8,128)S(1)}, s32[8,2048]{1,0:T(8,128)}, u32[]{:S(2)}) copy-start(s32[8,2048]{1,0:T(8,128)} %param.10) | copy-start | bytes 196612
  7.2 8.3 %copy-start.1 = (f32[8,2048]{1,0:T(8,128)S(1)}, f32[8,2048]{1,0:T(8,128)}, u32[]{:S(2)}) copy-start(f32[8,2048]{1,0:T(8,128)} %param.11) | copy-start | bytes 196612
  7.2 8.3 %copy-start.5 = (s32[8]{0:T(128)S(1)}, s32[8]{0:T(128)}, u32[]{:S(2)}) copy-start(s32[8]{0:T(128)} %param.14) | copy-start | bytes 100
  7.2 8.3 %copy-start.3 = (f32[8,2048]{1,0:T(8,128)S(1)}, f32[8,2048]{1,0:T(8,128)}, u32[]{:S(2)}) copy-start(f32[8,2048]{1,0:T(8,128)} %param.9) | copy-start | bytes 196612
  7.2 52.8 %reduce-scatter.3.cloned.1.call-start = ((), (), s32[]{:S(2)}) async-start(), calls=%async_computation.2 | async-start | bytes 2621440 | tf_op jit(solution)/shard_map/reduce_scatter | solution.py:73
  9.7 6.0 %copy-start = (bf16[8,2048,256]{2,1,0:T(8,128)(2,1)S(1)}, bf16[8,2048,256]{2,1,0:T(8,128)(2,1)}, u32[]{:S(2)}) copy-start(bf16[8,2048,256]{2,1,0:T(8,128)(2,1)} %param.8) | copy-start | bytes 25165828
  15.7 45.7 %copy-start.4 = (s32[256]{0:T(256)S(1)}, s32[256]{0:T(256)}, u32[]{:S(2)}) copy-start(s32[256]{0:T(256)} %param.15) | copy-start | bytes 3076
  26.0 109.0 %all-gather.2.cloned.1.call-start = ((), (), s32[]{:S(2)}) async-start(), calls=%async_computation.3 | async-start | bytes 4718592 | tf_op jit(solution)/shard_map/all_gather | solution.py:89
  60.1 419.5 %reduce-scatter.5.cloned.1.call-start = ((), (), s32[]{:S(2)}) async-start(), calls=%async_computation.4 | async-start | bytes 41943040 | tf_op jit(solution)/shard_map/reduce_scatter | solution.py:99
  248.0 4.6 copy-start.6
Sparse Core Ops, SparseCore 0:
  26.1 33.9 reduce-scatter.2
  62.2 72.7 all-gather.1
  248.1 231.4 reduce-scatter.4
where the time goes:
time: 496 us; the launch traced here: 495 us
  waiting for transfers between devices  284 us (57%)
  local copies, waits for them, and re-layouts  105 us (21%)
  blocking collectives  45.1 us (9%)
  other arithmetic  24.6 us (5%)
  matrix products  20.9 us (4%)
  between operations  14.7 us (3%)
    reduce_scatter x1, waiting for transfers between devices, local(): lax.psum_scatter(tiles_part, 'bins', scatter_dimension=0, tiled=True)  178 us
    all_gather x1, waiting for transfers between devices, local(): every_blocks = lax.all_gather(mine_blocks, 'chan', axis=0, tiled=True)  71.4 us
    unnamed x2, blocking collectives  45.1 us
    reshape x1, local copies, waits for them, and re-layouts, place_blocks(): jnp.transpose(placed_buffer, (0, 1, 3, 2, 4))  39.2 us
    transpose x1, local copies, waits for them, and re-layouts, place_blocks(): jnp.transpose(placed_buffer, (0, 1, 3, 2, 4))  37.8 us
    reduce_scatter x1, waiting for transfers between devices, local(): lax.psum_scatter(blocks, 'bins', scatter_dimension=0, tiled=True)  34 us
    scatter-add x1, other arithmetic, place_blocks(): placed_buffer.at[slot_ids, row_offset, col_offset]  14.2 us
    broadcast_in_dim x1, local copies, waits for them, and re-layouts, place_blocks(): jnp.zeros((slot_count, per_tile, per_tile, run_width, run_width), jnp.flo...  11.2 us
  transfers between devices with their start and end apart: 3, of which 3 were waited for; matrix products, arithmetic and copies ran while one was open for 2% of the time, Pallas kernels for 0%

commit v1 on v0

v1 whole, which is shorter than its diff:
```python
import functools

import jax
import jax.numpy as jnp
from jax import lax
from jax.experimental import pallas as pl
from jax.experimental.pallas import tpu as pltpu
from jax.sharding import PartitionSpec as P

GW = 128
TILE = 512
EXTRA = 8


def channel_payload(eff, chosen, nominal, observed, variance, live):
    eff_t = eff.T
    exponent = jnp.dot(chosen, eff_t, preferred_element_type=jnp.float32)[0:8]
    expected = nominal * jnp.exp(exponent)
    denominator = 1.0 + expected * variance
    residual = jnp.where(live, (expected - observed) / denominator, 0.0)
    weight = jnp.where(live, expected / denominator, 0.0)
    weighted = (eff_t.astype(jnp.float32) * weight[0:1]).astype(jnp.bfloat16)
    residual_rows = jnp.concatenate([residual, residual], axis=0).astype(jnp.bfloat16)
    left = jnp.concatenate([weighted, residual_rows], axis=0)
    full = jnp.dot(left, eff, preferred_element_type=jnp.float32)
    first, off, second = full[:GW, :GW], full[:GW, GW:], full[GW : 2 * GW, GW:]
    row = lax.broadcasted_iota(jnp.int32, (GW, GW), 0)
    col = lax.broadcasted_iota(jnp.int32, (GW, GW), 1)
    packed = jnp.where(row <= col, first, second)
    second_diag = jnp.sum(jnp.where(row == col, second, 0.0), axis=0, keepdims=True)
    grad0 = full[2 * GW : 2 * GW + 8, :GW]
    grad1 = full[2 * GW : 2 * GW + 8, GW:]
    which = lax.broadcasted_iota(jnp.int32, (EXTRA, GW), 0)
    extra = jnp.where(
        which == 0, grad0, jnp.where(which == 1, grad1, jnp.broadcast_to(second_diag, (EXTRA, GW)))
    )
    return packed, off, extra


def curvature_kernel(groups_ref, counts_ref, eff_ref, nom_ref, obs_ref, var_ref, theta_ref, out_ref):
    chan = lax.axis_index("chan")
    bins = lax.axis_index("bins")
    c = pl.program_id(0)
    size = eff_ref.shape[1]
    base = chan * pl.num_programs(0) + c
    g0, g1 = groups_ref[base, 0], groups_ref[base, 1]
    chosen = jnp.concatenate([theta_ref[g0], theta_ref[g1]], axis=1).astype(jnp.bfloat16)
    chosen = jnp.broadcast_to(chosen, (16, 2 * GW))
    nominal, observed, variance = nom_ref[c], obs_ref[c].astype(jnp.float32), var_ref[c]
    position = bins * size + lax.broadcasted_iota(jnp.int32, (8, size), 1)
    packed, off, extra = channel_payload(
        eff_ref[0], chosen, nominal, observed, variance, position < counts_ref[c]
    )
    out_ref[0, :GW] = packed
    out_ref[0, GW : 2 * GW] = off
    out_ref[0, 2 * GW :] = extra


def curvature(effects, nominal, observed, variance, theta, groups, counts):
    chans, size, width = effects.shape
    rows = 2 * GW + EXTRA
    whole = lambda *shape: pl.BlockSpec(shape, lambda c, *_: (0,) * len(shape))
    return pl.pallas_call(
        curvature_kernel,
        grid_spec=pltpu.PrefetchScalarGridSpec(
            num_scalar_prefetch=2,
            grid=(chans,),
            in_specs=[
                pl.BlockSpec((1, size, width), lambda c, *_: (c, 0, 0)),
                whole(chans, 1, size),
                whole(chans, 1, size),
                whole(chans, 1, size),
                whole(theta.shape[0] // GW, 1, GW),
            ],
            out_specs=pl.BlockSpec((1, rows, GW), lambda c, *_: (c, 0, 0)),
        ),
        out_shape=jax.ShapeDtypeStruct((chans, rows, GW), jnp.float32),
        compiler_params=pltpu.CompilerParams(vmem_limit_bytes=40 * 2**20),
        name="curvature",
    )(
        groups,
        counts,
        effects,
        nominal.reshape(chans, 1, size),
        observed.reshape(chans, 1, size),
        variance.reshape(chans, 1, size),
        theta.reshape(-1, 1, GW),
    )


def place_kernel(
    groups_ref, owner_ref, payload_ref, theta_ref, tiles_ref, grad_ref,
    held, grads, lookup, entries, counts, waited, held_sem, grad_sem,
):
    step = pl.program_id(0)
    slots = pl.num_programs(0)
    device = lax.axis_index("chan") * lax.axis_size("bins") + lax.axis_index("bins")
    chans = payload_ref.shape[0]
    per_tile = TILE // GW
    total_groups = theta_ref.shape[0]
    side = total_groups // per_tile
    room = entries.shape[0] // counts.shape[0]
    start = device * slots

    def copy_of(c):
        return pltpu.make_async_copy(
            payload_ref.at[c, pl.ds(0, 2 * GW + EXTRA)], held.at[c], held_sem.at[c]
        )

    grad_copy = pltpu.make_async_copy(
        payload_ref.at[:, pl.ds(2 * GW, EXTRA)], grads, grad_sem.at[0]
    )

    @pl.when(step == 0)
    def _():
        grad_copy.start()

        def clear(i, _):
            for j in range(16):
                lookup[i * 16 + j] = -1
            return 0

        lax.fori_loop(0, side * side // 16, clear, 0)
        for s in range(counts.shape[0]):
            counts[s] = 0
            lookup[owner_ref[start + s]] = s

        def visit(c, _):
            a, b = groups_ref[c, 0], groups_ref[c, 1]
            ta, tb = a // per_tile, b // per_tile
            ra, rb = a % per_tile, b % per_tile
            hits = []
            for kind, (tr, tc, rr, rc) in enumerate(
                ((ta, ta, ra, ra), (tb, tb, rb, rb), (ta, tb, ra, rb), (tb, ta, rb, ra))
            ):
                slot = lookup[tr * side + tc]
                hits.append(slot)

                @pl.when(slot >= 0)
                def _(slot=slot, kind=kind, rr=rr, rc=rc):
                    n = counts[slot]
                    entries[slot * room + n] = ((c * per_tile + rr) * per_tile + rc) * 4 + kind
                    counts[slot] = n + 1

            used = jnp.maximum(jnp.maximum(hits[0], hits[1]), jnp.maximum(hits[2], hits[3])) >= 0
            waited[c] = jnp.where(used, 0, 1)

            @pl.when(used)
            def _():
                copy_of(c).start()

            return 0

        lax.fori_loop(0, chans, visit, 0)

    tile = owner_ref[start + step]

    tiles_ref[...] = jnp.zeros_like(tiles_ref)
    eye = (
        lax.broadcasted_iota(jnp.int32, (GW, GW), 0) == lax.broadcasted_iota(jnp.int32, (GW, GW), 1)
    ).astype(jnp.float32)

    @pl.when(tile // side == tile % side)
    def _():
        for r in range(per_tile):
            tiles_ref[0, r * GW : (r + 1) * GW, r * GW : (r + 1) * GW] = eye

    row = lax.broadcasted_iota(jnp.int32, (GW, GW), 0)
    col = lax.broadcasted_iota(jnp.int32, (GW, GW), 1)

    def accumulate(i, _):
        code = entries[step * room + i]
        kind = code % 4
        rc = code // 4 % per_tile
        rr = code // (4 * per_tile) % per_tile
        c = code // (4 * per_tile * per_tile)

        @pl.when(waited[c] == 0)
        def _():
            copy_of(c).wait()
            waited[c] = 1

        at = (
            0,
            pl.ds(pl.multiple_of(rr * GW, GW), GW),
            pl.ds(pl.multiple_of(rc * GW, GW), GW),
        )

        @pl.when(kind == 0)
        def _():
            upper = jnp.where(row <= col, held[c, :GW], 0.0)
            tiles_ref[at] += upper + jnp.where(row > col, upper.T, 0.0)

        @pl.when(kind == 1)
        def _():
            lower = jnp.where(row > col, held[c, :GW], 0.0)
            diag = jnp.where(row == col, held[c, 2 * GW + 2 : 2 * GW + 3], 0.0)
            tiles_ref[at] += lower + lower.T + diag

        @pl.when(kind == 2)
        def _():
            tiles_ref[at] += held[c, GW : 2 * GW]

        @pl.when(kind == 3)
        def _():
            tiles_ref[at] += held[c, GW : 2 * GW].T

        return 0

    lax.fori_loop(0, counts[step], accumulate, 0)

    @pl.when(step == slots - 1)
    def _():
        grad_copy.wait()
        mine = grad_ref.shape[0]
        first = device * total_groups // (lax.axis_size("chan") * lax.axis_size("bins"))
        for m in range(mine):
            grad_ref[m] = theta_ref[first + m]

        def add(c, _):
            for r in range(2):
                m = groups_ref[c, r] - first

                @pl.when(jnp.logical_and(m >= 0, m < mine))
                def _(m=m, r=r):
                    grad_ref[m] += grads[c, r : r + 1]

            return 0

        lax.fori_loop(0, chans, add, 0)


def place(payload, theta, groups, tile_owner, slots, mine):
    chans, rows = payload.shape[:2]
    return pl.pallas_call(
        place_kernel,
        grid_spec=pltpu.PrefetchScalarGridSpec(
            num_scalar_prefetch=2,
            grid=(slots,),
            in_specs=[
                pl.BlockSpec(memory_space=pl.ANY),
                pl.BlockSpec((theta.shape[0] // GW, 1, GW), lambda s, *_: (0, 0, 0)),
            ],
            out_specs=[
                pl.BlockSpec((1, TILE, TILE), lambda s, *_: (s, 0, 0)),
                pl.BlockSpec((mine, 1, GW), lambda s, *_: (0, 0, 0)),
            ],
            scratch_shapes=[
                pltpu.VMEM((chans, rows, GW), jnp.float32),
                pltpu.VMEM((chans, EXTRA, GW), jnp.float32),
                pltpu.SMEM((tile_owner.shape[0],), jnp.int32),
                pltpu.SMEM((slots * chans * 4,), jnp.int32),
                pltpu.SMEM((slots,), jnp.int32),
                pltpu.SMEM((chans,), jnp.int32),
                pltpu.SemaphoreType.DMA((chans,)),
                pltpu.SemaphoreType.DMA((1,)),
            ],
        ),
        out_shape=[
            jax.ShapeDtypeStruct((slots, TILE, TILE), jnp.float32),
            jax.ShapeDtypeStruct((mine, 1, GW), jnp.float32),
        ],
        compiler_params=pltpu.CompilerParams(vmem_limit_bytes=50 * 2**20),
        name="place",
    )(groups, tile_owner, payload, theta.reshape(-1, 1, GW))


def local(effects, nominal, observed, mc_variance, theta, nuisance_index, bin_counts, tile_owner):
    devices = lax.axis_size("chan") * lax.axis_size("bins")
    device = lax.axis_index("chan") * lax.axis_size("bins") + lax.axis_index("bins")
    total_nu = theta.shape[0]
    slice_len = total_nu // devices
    groups = nuisance_index[:, ::GW] // GW
    parts = curvature(effects, nominal, observed, mc_variance, theta, groups, bin_counts)
    summed = lax.psum_scatter(parts, "bins", scatter_dimension=0, tiled=True)
    payload = lax.all_gather(summed, ("chan", "bins"), axis=0, tiled=True)
    tiles, grad = place(
        payload, theta, groups, tile_owner, tile_owner.shape[0] // devices, max(1, slice_len // GW)
    )
    gradient = grad.reshape(-1)
    if slice_len < GW:
        gradient = lax.dynamic_slice_in_dim(gradient, device * slice_len % GW, slice_len, 0)
    return (tiles, gradient)


def solution(mesh):
    return jax.shard_map(
        local,
        mesh=mesh,
        in_specs=(
            P("chan", "bins", None),
            P("chan", "bins"),
            P("chan", "bins"),
            P("chan", "bins"),
            P(),
            P(),
            P("chan"),
            P(),
        ),
        out_specs=(P(("chan", "bins"), None, None), P(("chan", "bins"))),
        check_vma=False,
    )
```

time: 496 us -> 154 us (0.31)
  waiting for transfers between devices: 284 us -> 109 us
  local copies, waits for them, and re-layouts: 105 us -> 8.38 us
  blocking collectives: 45.1 us -> 0 us
  other arithmetic: 24.6 us -> 0.03 us
  matrix products: 20.9 us -> 0 us
  Pallas kernels: 0 us -> 20 us
    reduce_scatter x2 -> x1, waiting for transfers between devices: 212 us -> 27.8 us  [local(): summed = lax.psum_scatter(parts, 'bins', scatter_dimension=0, tiled=True)]
    unnamed x2 -> x0, blocking collectives: 45.1 us -> none
    transpose x2 -> x0, local copies, waits for them, and re-layouts: 42.6 us -> none  [the longest x1 37.8 us: place_blocks(): jnp.transpose(placed_buffer, (0, 1, 3, 2, 4))]
    reshape x3, local copies, waits for them, and re-layouts: 44.9 us -> 2.66 us  [the longest x1 0.89 us: curvature(): nominal.reshape(chans, 1, size)]
    dot_general x4 -> x0, matrix products: 20.9 us -> none  [the longest x1 10.3 us: local(): jnp.einsum('cbk,cbl->ckl', scaled, scaled, preferred_element_type=jnp.flo...]
    pallas_call x0 -> x2, Pallas kernels: none -> 20 us  [the longest x1 11 us: place(): pl.pallas_call(place_kernel, grid_spec=pltpu.PrefetchScalarGridSpec(num_s...]
    scatter-add x1 -> x0, other arithmetic: 14.2 us -> none  [place_blocks(): placed_buffer.at[slot_ids, row_offset, col_offset]]
    broadcast_in_dim x2 -> x0, local copies, waits for them, and re-layouts: 11.3 us -> none  [the longest x1 11.2 us: place_blocks(): jnp.zeros((slot_count, per_tile, per_tile, run_width, run_width), jnp.flo...]
  transfers between devices with their start and end apart: 3 -> 2, of which waited for: 3 -> 2; matrix products, arithmetic and copies ran while one was open for 2% -> 0% of each run, Pallas kernels for 0% -> 0%
where the time goes in v1:
time: 154 us; the launch traced here: 151 us
  waiting for transfers between devices  109 us (71%)
  Pallas kernels  20 us (13%)
  between operations  14.1 us (9%)
  local copies, waits for them, and re-layouts  8.38 us (5%)
    all_gather x1, waiting for transfers between devices, local(): payload = lax.all_gather(summed, ('chan', 'bins'), axis=0, tiled=True)  81 us
    reduce_scatter x1, waiting for transfers between devices, local(): summed = lax.psum_scatter(parts, 'bins', scatter_dimension=0, tiled=True)  27.8 us
    pallas_call x1, Pallas kernels, place(): pl.pallas_call(place_kernel, grid_spec=pltpu.PrefetchScalarGridSpec(num_s...  11 us
    pallas_call x1, Pallas kernels, curvature(): pl.pallas_call(curvature_kernel, grid_spec=pltpu.PrefetchScalarGridSpec(n...  8.96 us
    unnamed x10, local copies, waits for them, and re-layouts  4.8 us
  transfers between devices with their start and end apart: 2, of which 2 were waited for; matrix products, arithmetic and copies ran while one was open for 0% of the time, Pallas kernels for 0%

profile of v1, /device:TPU:0, one launch (start us, length us, event | category | flops | bytes accessed | tf_op | source)
XLA Modules:
  0.0 151.4 jit_solution(3868327594284013069)
XLA Ops:
  7.2 0.0 copy-start.2
  7.2 0.0 copy-start.3
  7.2 0.0 reduce-scatter.2.cloned.1.call-start
  7.2 0.9 slice.3
  8.2 0.9 reshape.20.nom_ref
  9.1 0.9 reshape.21.obs_ref
  10.0 0.9 reshape.22.var_ref
  10.9 0.0 copy-start
  10.9 3.4 %copy-done = bf16[8,2048,256]{2,1,0:T(8,128)(2,1)S(1)} copy-done((bf16[8,2048,256]{2,1,0:T(8,128)(2,1)S(1)}, bf16[8,2048,256]{2,1,0:T(8,128)(2,1)}, u32[]{:S(2)}) %copy-start) | copy-done | bytes 8388632
  14.2 0.0 copy-start.1
  14.2 0.8 copy-done.1
  15.0 0.0 copy-start.4
  15.0 0.7 copy-done.4
  15.7 9.0 %curvature.1 = f32[8,264,128]{2,1,0:T(8,128)} custom-call(s32[64,2]{1,0:T(8,128)S(1)} %add_select_fusion.groups_ref, s32[8]{0:T(128)S(1)} %copy-done.4, bf16[8,2048,256]{2,1,0:T(8,128)(2,1)S(1)} %copy-done, f32[8,1,2048]{2,1,0:T(1,128)S(1)} %reshape.20.nom_ref, s32[8,1,2048]{2,1,0:T(1,128)S(1)} %reshape.21.obs_ref, f32[8,1,2048]{2,1,0:T(1,128)S(1)} %reshape.22.var_ref, ...), custom_call_target="tpu_custom_call" | custom-call | tf_op jit(solution)/shard_map/curvature/pallas_call | solution.py:63
  24.6 0.0 reduce-scatter.2.cloned.1.call-update
  24.6 0.0 all-gather.2.cloned.1.call-start
  24.7 27.8 %reduce-scatter.2.cloned.1.call-done = f32[2,264,128]{2,1,0:T(8,128)} async-done(((f32[8,264,128]{2,1,0:T(8,128)}), f32[2,264,128]{2,1,0:T(8,128)}) %reduce-scatter.2.cloned.1.call-update) | async-done | bytes 270352 | tf_op jit(solution)/shard_map/reduce_scatter | solution.py:275
  52.5 0.0 all-gather.2.cloned.1.call-update
  52.5 81.0 %all-gather.2.cloned.1.call-done.payload_ref = f32[64,264,128]{2,1,0:T(8,128)} async-done(((f32[2,264,128]{2,1,0:T(8,128)}), f32[64,264,128]{2,1,0:T(8,128)}) %all-gather.2.cloned.1.call-update) | async-done | bytes 8650768 | tf_op jit(solution)/shard_map/all_gather | solution.py:276
  133.5 0.0 copy-done.2
  133.5 0.0 copy-done.3
  133.5 11.0 %place.1 = (f32[8,512,512]{2,1,0:T(8,128)}, f32[2,1,128]{2,1,0:T(1,128)}) custom-call(s32[64,2]{1,0:T(8,128)S(1)} %add_select_fusion.groups_ref, s32[256]{0:T(256)S(1)} %copy-done.3, f32[64,264,128]{2,1,0:T(8,128)} %all-gather.2.cloned.1.call-done.payload_ref, f32[64,1,128]{2,1,0:T(1,128)S(1)} %bitcast.3), custom_call_target="tpu_custom_call" | custom-call | tf_op jit(solution)/shard_map/place/pallas_call | solution.py:235
  (1 shorter events, 0.0 us)
Async XLA Ops:
  7.2 126.3 %copy-start.2 = (f32[8192]{0:T(1024)S(1)}, f32[8192]{0:T(1024)}, u32[]{:S(2)}) copy-start(f32[8192]{0:T(1024)} %param.12) | copy-start | bytes 98308
  7.2 126.3 %copy-start.3 = (s32[256]{0:T(256)S(1)}, s32[256]{0:T(256)}, u32[]{:S(2)}) copy-start(s32[256]{0:T(256)} %owner_ref.1) | copy-start | bytes 3076
  7.2 45.3 %reduce-scatter.2.cloned.1.call-start = ((), (), s32[]{:S(2)}) async-start(), calls=%async_computation.1 | async-start | bytes 1351680 | tf_op jit(solution)/shard_map/reduce_scatter | solution.py:275
  10.9 3.4 %copy-start = (bf16[8,2048,256]{2,1,0:T(8,128)(2,1)S(1)}, bf16[8,2048,256]{2,1,0:T(8,128)(2,1)}, u32[]{:S(2)}) copy-start(bf16[8,2048,256]{2,1,0:T(8,128)(2,1)} %eff_ref.1) | copy-start | bytes 25165828
  14.2 0.8 copy-start.1
  15.0 0.7 copy-start.4
  24.6 108.8 %all-gather.2.cloned.1.call-start = ((), (), s32[]{:S(2)}) async-start(), calls=%async_computation.2 | async-start | bytes 8921088 | tf_op jit(solution)/shard_map/all_gather | solution.py:276
Sparse Core Ops, SparseCore 0:
  24.8 27.6 reduce-scatter.1
  55.4 78.0 all-gather.1

commit v2 on v1

--- a/solution.py
+++ b/solution.py
@@ -46,7 +46,8 @@
     g0, g1 = groups_ref[base, 0], groups_ref[base, 1]
     chosen = jnp.concatenate([theta_ref[g0], theta_ref[g1]], axis=1).astype(jnp.bfloat16)
     chosen = jnp.broadcast_to(chosen, (16, 2 * GW))
-    nominal, observed, variance = nom_ref[c], obs_ref[c].astype(jnp.float32), var_ref[c]
+    line = pl.ds(c, 1)
+    nominal, observed, variance = nom_ref[line], obs_ref[line].astype(jnp.float32), var_ref[line]
     position = bins * size + lax.broadcasted_iota(jnp.int32, (8, size), 1)
     packed, off, extra = channel_payload(
         eff_ref[0], chosen, nominal, observed, variance, position < counts_ref[c]
@@ -67,23 +68,23 @@
             grid=(chans,),
             in_specs=[
                 pl.BlockSpec((1, size, width), lambda c, *_: (c, 0, 0)),
-                whole(chans, 1, size),
-                whole(chans, 1, size),
-                whole(chans, 1, size),
+                whole(chans, size),
+                whole(chans, size),
+                whole(chans, size),
                 whole(theta.shape[0] // GW, 1, GW),
             ],
             out_specs=pl.BlockSpec((1, rows, GW), lambda c, *_: (c, 0, 0)),
         ),
         out_shape=jax.ShapeDtypeStruct((chans, rows, GW), jnp.float32),
-        compiler_params=pltpu.CompilerParams(vmem_limit_bytes=40 * 2**20),
+        compiler_params=pltpu.CompilerParams(vmem_limit_bytes=58 * 2**20),
         name="curvature",
     )(
         groups,
         counts,
         effects,
-        nominal.reshape(chans, 1, size),
-        observed.reshape(chans, 1, size),
-        variance.reshape(chans, 1, size),
+        nominal,
+        observed,
+        variance,
         theta.reshape(-1, 1, GW),
     )
 
@@ -260,9 +261,164 @@
             jax.ShapeDtypeStruct((slots, TILE, TILE), jnp.float32),
             jax.ShapeDtypeStruct((mine, 1, GW), jnp.float32),
         ],
-        compiler_params=pltpu.CompilerParams(vmem_limit_bytes=50 * 2**20),
+        compiler_params=pltpu.CompilerParams(
+            vmem_limit_bytes=4 * chans * (rows + EXTRA) * GW + 8 * 2**20
+        ),
         name="place",
     )(groups, tile_owner, payload, theta.reshape(-1, 1, GW))
+
+
+COLORS = ((0, 104, "zxy"), (104, 104, "zyx"), (208, 56, "xyz"))
+DEEP = 4
+
+
+def exchange_kernel(ydim, parts_ref, out_ref, swap, cross, total, swap_recv, cross_recv, recv, drecv, send):
+    chan, bins = lax.axis_index("chan"), lax.axis_index("bins")
+    zdim = lax.axis_size("chan") // ydim
+    nbins = lax.axis_size("bins")
+    z, y = chan // ydim, chan % ydim
+    x, core = bins // 2, bins % 2
+    held = parts_ref.shape[0] // nbins
+    issued = []
+
+    def device(zz, yy, xx, kk):
+        return {"chan": zz * ydim + yy, "bins": xx * 2 + kk}
+
+    def copy(src, dst, recv_sem, target, cond=None):
+        made = pltpu.make_async_remote_copy(
+            src_ref=src,
+            dst_ref=dst,
+            send_sem=send.at[len(issued)],
+            recv_sem=recv_sem,
+            device_id=target,
+            device_id_type=pl.DeviceIdType.MESH,
+        )
+        issued.append((made, cond))
+        run(cond, made.start)
+
+    def run(cond, action):
+        if cond is None:
+            action()
+        else:
+            pl.when(cond)(action)
+
+    partner = device(z, y, x, 1 - core)
+    beside = device(z, y, 1 - x, core)
+    below_there, above_there = z > 0, z < zdim - 1
+
+    barrier = pltpu.get_barrier_semaphore()
+    for target, cond in (
+        (partner, None),
+        (beside, None),
+        (device(z, 1 - y, x, core), None),
+        (device(z - 1, y, x, core), below_there),
+        (device(z + 1, y, x, core), above_there),
+    ):
+        run(cond, lambda target=target: pl.semaphore_signal(
+            barrier, 1, device_id=target, device_id_type=pl.DeviceIdType.MESH
+        ))
+    pl.semaphore_wait(barrier, 3 + jnp.minimum(z, 1) + jnp.minimum(zdim - 1 - z, 1))
+
+    far, near = (1 - x) * 2, x * 2
+    for half, owner in enumerate((far, near)):
+        for i in range(held):
+            copy(
+                parts_ref.at[(owner + 1 - core) * held + i],
+                swap.at[half * held + i],
+                swap_recv.at[half * held + i],
+                partner,
+            )
+
+    def arrived(dst, sem):
+        pltpu.make_async_remote_copy(
+            src_ref=dst, dst_ref=dst, send_sem=send.at[0], recv_sem=sem,
+            device_id=partner, device_id_type=pl.DeviceIdType.MESH,
+        ).wait_recv()
+
+    for i in range(held):
+        arrived(swap.at[i], swap_recv.at[i])
+        total[i] = parts_ref[(far + core) * held + i] + swap[i]
+        copy(total.at[i], cross.at[i], cross_recv.at[i], beside)
+    base = bins * held + chan * nbins * held
+    for i in range(held):
+        arrived(swap.at[held + i], swap_recv.at[held + i])
+        arrived(cross.at[i], cross_recv.at[i])
+        out_ref[base + i] = (
+            parts_ref[(near + core) * held + i] + swap[held + i]
+        ) + cross[i]
+
+    events = []
+    for color, (_, _, order) in enumerate(COLORS):
+        for dz in range(1 - zdim, zdim):
+            for fx in range(2):
+                for fy in range(2):
+                    events.append((abs(dz) + fx + fy, fx + fy, color, dz, fx, fy))
+    events.sort()
+    for _, _, color, dz, fx, fy in events:
+        first, count, order = COLORS[color]
+        sz, sx, sy = z + dz, (1 - x if fx else x), (1 - y if fy else y)
+        chip = (sz * ydim + sy) * 2 + sx
+        there = None if dz == 0 else (z >= -dz if dz < 0 else z < zdim - dz)
+        at = ((sz * ydim + sy) * nbins + sx * 2 + core) * held
+        piece = out_ref.at[pl.ds(at, held), pl.ds(first, count)]
+        offset = {"z": dz, "x": fx, "y": fy}
+        last = max([n for n, d in enumerate(order) if offset[d]], default=-1)
+        sem = recv.at[color, chip]
+        if last >= 0:
+            run(there, lambda piece=piece, sem=sem: arrived(piece, sem))
+
+        def both(a, b):
+            return b if a is None else (a if b is None else jnp.logical_and(a, b))
+
+        if zdim > 1:
+            onward = order.index("z") > last
+            if (onward or (last >= 0 and order[last] == "z" and dz < 0)) and dz >= 2 - zdim:
+                copy(piece, piece, sem, device(z + 1, y, x, core), both(there, above_there))
+            if (onward or (last >= 0 and order[last] == "z" and dz > 0)) and dz <= zdim - 2:
+                copy(piece, piece, sem, device(z - 1, y, x, core), both(there, below_there))
+        if order.index("x") > last:
+            copy(piece, piece, sem, beside, there)
+        if order.index("y") > last:
+            copy(piece, piece, sem, device(z, 1 - y, x, core), there)
+        copy(piece, piece, drecv.at[color, chip], partner, there)
+
+    for color, (first, count, _) in enumerate(COLORS):
+        for chip in range(zdim * ydim * 2):
+            at = (chip // 2 * nbins + chip % 2 * 2 + 1 - core) * held
+            arrived(out_ref.at[pl.ds(at, held), pl.ds(first, count)], drecv.at[color, chip])
+    for made, cond in issued:
+        run(cond, made.wait_send)
+
+
+def exchange(parts):
+    nbins, nchan = lax.axis_size("bins"), lax.axis_size("chan")
+    chans, rows, width = parts.shape
+    held = chans // nbins
+    whole = pl.BlockSpec(memory_space=pltpu.VMEM)
+    chips = nchan * nbins // 2
+    return pl.pallas_call(
+        functools.partial(exchange_kernel, 2),
+        in_specs=[whole],
+        out_specs=whole,
+        out_shape=jax.ShapeDtypeStruct((nchan * chans, rows, width), jnp.float32),
+        scratch_shapes=[
+            pltpu.VMEM((2 * held, rows, width), jnp.float32),
+            pltpu.VMEM((held, rows, width), jnp.float32),
+            pltpu.VMEM((held, rows, width), jnp.float32),
+            pltpu.SemaphoreType.DMA((2 * held,)),
+            pltpu.SemaphoreType.DMA((held,)),
+            pltpu.SemaphoreType.DMA((len(COLORS), chips)),
+            pltpu.SemaphoreType.DMA((len(COLORS), chips)),
+            pltpu.SemaphoreType.DMA((SENDS,)),
+        ],
+        compiler_params=pltpu.CompilerParams(
+            collective_id=0, has_side_effects=True, vmem_limit_bytes=32 * 2**20
+        ),
+        name="exchange",
+    )(parts)
+
+
+SENDS = 240
 
 
 def local(effects, nominal, observed, mc_variance, theta, nuisance_index, bin_counts, tile_owner):
@@ -272,8 +428,12 @@
     slice_len = total_nu // devices
     groups = nuisance_index[:, ::GW] // GW
     parts = curvature(effects, nominal, observed, mc_variance, theta, groups, bin_counts)
-    summed = lax.psum_scatter(parts, "bins", scatter_dimension=0, tiled=True)
-    payload = lax.all_gather(summed, ("chan", "bins"), axis=0, tiled=True)
+    chan_size, bins_size = lax.axis_size("chan"), lax.axis_size("bins")
+    if bins_size == 4 and chan_size % 2 == 0 and chan_size // 2 <= DEEP:
+        payload = exchange(parts)
+    else:
+        summed = lax.psum_scatter(parts, "bins", scatter_dimension=0, tiled=True)
+        payload = lax.all_gather(summed, ("chan", "bins"), axis=0, tiled=True)
     tiles, grad = place(
         payload, theta, groups, tile_owner, tile_owner.shape[0] // devices, max(1, slice_len // GW)
     )

time: 154 us -> 84.3 us (0.55)
  waiting for transfers between devices: 109 us -> 0 us
  Pallas kernels: 20 us -> 79.5 us
  between operations: 14.1 us -> 0.67 us
  local copies, waits for them, and re-layouts: 8.38 us -> 2.17 us
    all_gather x1 -> x0, waiting for transfers between devices: 81 us -> none  [local(): payload = lax.all_gather(summed, ('chan', 'bins'), axis=0, tiled=True)]
    pallas_call x0 -> x1, Pallas kernels: none -> 54.1 us  [exchange(): pl.pallas_call(functools.partial(exchange_kernel, 2), in_specs=[whole], o...]
    reduce_scatter x1 -> x0, waiting for transfers between devices: 27.8 us -> none  [local(): summed = lax.psum_scatter(parts, 'bins', scatter_dimension=0, tiled=True)]
    unnamed x10 -> x8, local copies, waits for them, and re-layouts: 4.8 us -> 1.25 us
    pallas_call x1, Pallas kernels: 8.96 us -> 11.7 us  [curvature(): pl.pallas_call(curvature_kernel, grid_spec=pltpu.PrefetchScalarGridSpec(n...]
    pallas_call x1, Pallas kernels: 11 us -> 13.7 us  [place(): pl.pallas_call(place_kernel, grid_spec=pltpu.PrefetchScalarGridSpec(num_s...]
    reshape x3 -> x0, local copies, waits for them, and re-layouts: 2.66 us -> none  [the longest x1 0.89 us: curvature(): nominal.reshape(chans, 1, size)]
  transfers between devices with their start and end apart: 2 -> 0, of which waited for: 2 -> 0; matrix products, arithmetic and copies ran while one was open for 0% -> 0% of each run, Pallas kernels for 0% -> 0%
where the time goes in v2:
time: 84.3 us; the launch traced here: 82.9 us
  Pallas kernels  79.5 us (94%)
  local copies, waits for them, and re-layouts  2.17 us (3%)
    pallas_call x1, Pallas kernels, exchange(): pl.pallas_call(functools.partial(exchange_kernel, 2), in_specs=[whole], o...  54.1 us
    pallas_call x1, Pallas kernels, place(): pl.pallas_call(place_kernel, grid_spec=pltpu.PrefetchScalarGridSpec(num_s...  13.7 us
    pallas_call x1, Pallas kernels, curvature(): pl.pallas_call(curvature_kernel, grid_spec=pltpu.PrefetchScalarGridSpec(n...  11.7 us

profile of v2, /device:TPU:0, one launch (start us, length us, event | category | flops | bytes accessed | tf_op | source)
XLA Modules:
  0.0 82.9 jit_solution(15902520195906935141)
XLA Ops:
  0.6 0.9 %slice.3 = s32[64,2]{1,0:T(8,128)S(1)} slice(s32[64,256]{1,0:T(8,128)} %param.13), slice={[0:64:1], [0:256:128]} | slice | bytes 1024 | tf_op jit(solution)/shard_map/slice | solution.py:429
  1.6 0.6 add_select_fusion.groups_ref
  2.2 0.0 copy-start.1
  2.2 0.0 copy-start.2
  2.2 0.0 copy-start.3
  2.2 11.7 %curvature.1.parts_ref = f32[8,264,128]{2,1,0:T(8,128)} custom-call(s32[64,2]{1,0:T(8,128)} %add_select_fusion.groups_ref, s32[8]{0:T(128)} %counts_ref.1, bf16[8,2048,256]{2,1,0:T(8,128)(2,1)} %eff_ref.1, f32[8,2048]{1,0:T(8,128)} %nom_ref.1, s32[8,2048]{1,0:T(8,128)} %obs_ref.1, f32[8,2048]{1,0:T(8,128)} %var_ref.1, f32[64,1,128]{2,1,0:T(1,128)} %bitcast.2), custom_call_target="tpu_custom_call" | custom-call | tf_op jit(solution)/shard_map/curvature/pallas_call | solution.py:64
  13.9 0.0 copy-start
  13.9 1.2 %copy-done = f32[8,264,128]{2,1,0:T(8,128)S(1)} copy-done((f32[8,264,128]{2,1,0:T(8,128)S(1)}, f32[8,264,128]{2,1,0:T(8,128)}, u32[]{:S(2)}) %copy-start) | copy-done | bytes 1081368
  15.1 54.1 %exchange.1.payload_ref = f32[64,264,128]{2,1,0:T(8,128)S(1)} custom-call(f32[8,264,128]{2,1,0:T(8,128)S(1)} %copy-done), custom_call_target="tpu_custom_call" | custom-call | tf_op jit(solution)/shard_map/exchange/pallas_call | solution.py:399
  69.2 0.0 copy-done.1
  69.2 0.0 copy-done.2
  69.2 0.0 copy-done.3
  69.3 13.7 %place.1 = (f32[8,512,512]{2,1,0:T(8,128)}, f32[2,1,128]{2,1,0:T(1,128)}) custom-call(s32[64,2]{1,0:T(8,128)S(1)} %copy-done.1, s32[256]{0:T(256)S(1)} %copy-done.3, f32[64,264,128]{2,1,0:T(8,128)S(1)} %exchange.1.payload_ref, f32[64,1,128]{2,1,0:T(1,128)S(1)} %bitcast.3), custom_call_target="tpu_custom_call" | custom-call | tf_op jit(solution)/shard_map/place/pallas_call | solution.py:236
Async XLA Ops:
  2.2 67.0 %copy-start.1 = (s32[64,2]{1,0:T(8,128)S(1)}, s32[64,2]{1,0:T(8,128)}, u32[]{:S(2)}) copy-start(s32[64,2]{1,0:T(8,128)} %add_select_fusion.groups_ref) | copy-start | bytes 1540
  2.2 67.0 %copy-start.2 = (f32[8192]{0:T(1024)S(1)}, f32[8192]{0:T(1024)}, u32[]{:S(2)}) copy-start(f32[8192]{0:T(1024)} %param.12) | copy-start | bytes 98308
  2.2 67.1 %copy-start.3 = (s32[256]{0:T(256)S(1)}, s32[256]{0:T(256)}, u32[]{:S(2)}) copy-start(s32[256]{0:T(256)} %owner_ref.1) | copy-start | bytes 3076
  13.9 1.2 %copy-start = (f32[8,264,128]{2,1,0:T(8,128)S(1)}, f32[8,264,128]{2,1,0:T(8,128)}, u32[]{:S(2)}) copy-start(f32[8,264,128]{2,1,0:T(8,128)} %curvature.1.parts_ref) | copy-start | bytes 3244036

commit v3 on v2

--- a/solution.py
+++ b/solution.py
@@ -91,68 +91,46 @@
 
 def place_kernel(
     groups_ref, owner_ref, payload_ref, theta_ref, tiles_ref, grad_ref,
-    held, grads, lookup, entries, counts, waited, held_sem, grad_sem,
+    lookup, entries, counts,
 ):
     step = pl.program_id(0)
-    slots = pl.num_programs(0)
+    slots = counts.shape[0] - 1
     device = lax.axis_index("chan") * lax.axis_size("bins") + lax.axis_index("bins")
     chans = payload_ref.shape[0]
     per_tile = TILE // GW
     total_groups = theta_ref.shape[0]
     side = total_groups // per_tile
-    room = entries.shape[0] // counts.shape[0]
+    shift = per_tile.bit_length() - 1
+    room = 4 * chans
     start = device * slots
-
-    def copy_of(c):
-        return pltpu.make_async_copy(
-            payload_ref.at[c, pl.ds(0, 2 * GW + EXTRA)], held.at[c], held_sem.at[c]
-        )
-
-    grad_copy = pltpu.make_async_copy(
-        payload_ref.at[:, pl.ds(2 * GW, EXTRA)], grads, grad_sem.at[0]
-    )
 
     @pl.when(step == 0)
     def _():
-        grad_copy.start()
-
         def clear(i, _):
             for j in range(16):
-                lookup[i * 16 + j] = -1
+                lookup[i * 16 + j] = slots
             return 0
 
         lax.fori_loop(0, side * side // 16, clear, 0)
-        for s in range(counts.shape[0]):
+        counts[slots] = 0
+        for s in range(slots):
             counts[s] = 0
             lookup[owner_ref[start + s]] = s
 
-        def visit(c, _):
-            a, b = groups_ref[c, 0], groups_ref[c, 1]
-            ta, tb = a // per_tile, b // per_tile
-            ra, rb = a % per_tile, b % per_tile
-            hits = []
-            for kind, (tr, tc, rr, rc) in enumerate(
-                ((ta, ta, ra, ra), (tb, tb, rb, rb), (ta, tb, ra, rb), (tb, ta, rb, ra))
-            ):
-                slot = lookup[tr * side + tc]
-                hits.append(slot)
-
-                @pl.when(slot >= 0)
-                def _(slot=slot, kind=kind, rr=rr, rc=rc):
+        def visit(pair, _):
+            for c in (pair * 2, pair * 2 + 1):
+                a, b = groups_ref[c, 0], groups_ref[c, 1]
+                ta, tb = a >> shift, b >> shift
+                ra, rb = a & (per_tile - 1), b & (per_tile - 1)
+                cases = ((ta, ta, ra, ra), (tb, tb, rb, rb), (ta, tb, ra, rb), (tb, ta, rb, ra))
+                for kind, (tr, tc, rr, rc) in enumerate(cases):
+                    slot = lookup[tr * side + tc]
                     n = counts[slot]
-                    entries[slot * room + n] = ((c * per_tile + rr) * per_tile + rc) * 4 + kind
+                    entries[slot * room + n] = ((((c << shift) + rr) << shift) + rc) * 4 + kind
                     counts[slot] = n + 1
-
-            used = jnp.maximum(jnp.maximum(hits[0], hits[1]), jnp.maximum(hits[2], hits[3])) >= 0
-            waited[c] = jnp.where(used, 0, 1)
-
-            @pl.when(used)
-            def _():
-                copy_of(c).start()
-
             return 0
 
-        lax.fori_loop(0, chans, visit, 0)
+        lax.fori_loop(0, chans // 2, visit, 0)
 
     tile = owner_ref[start + step]
 
@@ -171,16 +149,10 @@
 
     def accumulate(i, _):
         code = entries[step * room + i]
-        kind = code % 4
-        rc = code // 4 % per_tile
-        rr = code // (4 * per_tile) % per_tile
-        c = code // (4 * per_tile * per_tile)
-
-        @pl.when(waited[c] == 0)
-        def _():
-            copy_of(c).wait()
-            waited[c] = 1
-
+        kind = code & 3
+        rc = (code >> 2) & (per_tile - 1)
+        rr = (code >> (2 + shift)) & (per_tile - 1)
+        c = code >> (2 + 2 * shift)
         at = (
             0,
             pl.ds(pl.multiple_of(rr * GW, GW), GW),
@@ -189,22 +161,22 @@
 
         @pl.when(kind == 0)
         def _():
-            upper = jnp.where(row <= col, held[c, :GW], 0.0)
+            upper = jnp.where(row <= col, payload_ref[c, :GW], 0.0)
             tiles_ref[at] += upper + jnp.where(row > col, upper.T, 0.0)
 
         @pl.when(kind == 1)
         def _():
-            lower = jnp.where(row > col, held[c, :GW], 0.0)
-            diag = jnp.where(row == col, held[c, 2 * GW + 2 : 2 * GW + 3], 0.0)
+            lower = jnp.where(row > col, payload_ref[c, :GW], 0.0)
+            diag = jnp.where(row == col, payload_ref[c, 2 * GW + 2 : 2 * GW + 3], 0.0)
             tiles_ref[at] += lower + lower.T + diag
 
         @pl.when(kind == 2)
         def _():
-            tiles_ref[at] += held[c, GW : 2 * GW]
+            tiles_ref[at] += payload_ref[c, GW : 2 * GW]
 
         @pl.when(kind == 3)
         def _():
-            tiles_ref[at] += held[c, GW : 2 * GW].T
+            tiles_ref[at] += payload_ref[c, GW : 2 * GW].T
 
         return 0
 
@@ -212,7 +184,6 @@
 
     @pl.when(step == slots - 1)
     def _():
-        grad_copy.wait()
         mine = grad_ref.shape[0]
         first = device * total_groups // (lax.axis_size("chan") * lax.axis_size("bins"))
         for m in range(mine):
@@ -224,7 +195,7 @@
 
                 @pl.when(jnp.logical_and(m >= 0, m < mine))
                 def _(m=m, r=r):
-                    grad_ref[m] += grads[c, r : r + 1]
+                    grad_ref[m] += payload_ref[c, 2 * GW + r : 2 * GW + r + 1]
 
             return 0
 
@@ -239,7 +210,7 @@
             num_scalar_prefetch=2,
             grid=(slots,),
             in_specs=[
-                pl.BlockSpec(memory_space=pl.ANY),
+                pl.BlockSpec(memory_space=pltpu.VMEM),
                 pl.BlockSpec((theta.shape[0] // GW, 1, GW), lambda s, *_: (0, 0, 0)),
             ],
             out_specs=[
@@ -247,14 +218,9 @@
                 pl.BlockSpec((mine, 1, GW), lambda s, *_: (0, 0, 0)),
             ],
             scratch_shapes=[
-                pltpu.VMEM((chans, rows, GW), jnp.float32),
-                pltpu.VMEM((chans, EXTRA, GW), jnp.float32),
                 pltpu.SMEM((tile_owner.shape[0],), jnp.int32),
-                pltpu.SMEM((slots * chans * 4,), jnp.int32),
-                pltpu.SMEM((slots,), jnp.int32),
-                pltpu.SMEM((chans,), jnp.int32),
-                pltpu.SemaphoreType.DMA((chans,)),
-                pltpu.SemaphoreType.DMA((1,)),
+                pltpu.SMEM(((slots + 1) * chans * 4,), jnp.int32),
+                pltpu.SMEM((slots + 1,), jnp.int32),
             ],
         ),
         out_shape=[
@@ -272,7 +238,10 @@
 DEEP = 4
 
 
-def exchange_kernel(ydim, parts_ref, out_ref, swap, cross, total, swap_recv, cross_recv, recv, drecv, send):
+def exchange_kernel(
+    ydim, groups_ref, counts_ref, eff_ref, nom_ref, obs_ref, var_ref, theta_ref, out_ref,
+    eff_held, parts_ref, swap, cross, total, eff_sem, swap_recv, cross_recv, recv, drecv, send,
+):
     chan, bins = lax.axis_index("chan"), lax.axis_index("bins")
     zdim = lax.axis_size("chan") // ydim
     nbins = lax.axis_size("bins")
@@ -317,17 +286,44 @@
         run(cond, lambda target=target: pl.semaphore_signal(
             barrier, 1, device_id=target, device_id_type=pl.DeviceIdType.MESH
         ))
-    pl.semaphore_wait(barrier, 3 + jnp.minimum(z, 1) + jnp.minimum(zdim - 1 - z, 1))
-
     far, near = (1 - x) * 2, x * 2
-    for half, owner in enumerate((far, near)):
+    owners = (far + 1 - core, far + core, near + 1 - core, near + core)
+    size = eff_ref.shape[1]
+
+    def load(q, i):
+        at = q * held + i
+        return pltpu.make_async_copy(eff_ref.at[owners[q] * held + i], eff_held.at[at], eff_sem.at[at])
+
+    for q in range(4):
         for i in range(held):
-            copy(
-                parts_ref.at[(owner + 1 - core) * held + i],
-                swap.at[half * held + i],
-                swap_recv.at[half * held + i],
-                partner,
+            load(q, i).start()
+
+    def compute(q):
+        for i in range(held):
+            load(q, i).wait()
+
+        def one(i, _):
+            c = owners[q] * held + i
+            base = chan * nbins * held + c
+            g0, g1 = groups_ref[base, 0], groups_ref[base, 1]
+            chosen = jnp.concatenate([theta_ref[g0], theta_ref[g1]], axis=1).astype(jnp.bfloat16)
+            chosen = jnp.broadcast_to(chosen, (16, 2 * GW))
+            line = pl.ds(c, 1)
+            position = bins * size + lax.broadcasted_iota(jnp.int32, (8, size), 1)
+            packed, off, extra = channel_payload(
+                eff_held[q * held + i],
+                chosen,
+                nom_ref[line],
+                obs_ref[line].astype(jnp.float32),
+                var_ref[line],
+                position < counts_ref[c],
             )
+            parts_ref[q * held + i, :GW] = packed
+            parts_ref[q * held + i, GW : 2 * GW] = off
+            parts_ref[q * held + i, 2 * GW :] = extra
+            return 0
+
+        lax.fori_loop(0, held, one, 0)
 
     def arrived(dst, sem):
         pltpu.make_async_remote_copy(
@@ -335,17 +331,27 @@
             device_id=partner, device_id_type=pl.DeviceIdType.MESH,
         ).wait_recv()
 
+    def to_partner(q):
+        for i in range(held):
+            n = q // 2 * held + i
+            copy(parts_ref.at[q * held + i], swap.at[n], swap_recv.at[n], partner)
+
+    compute(0)
+    pl.semaphore_wait(barrier, 3 + jnp.minimum(z, 1) + jnp.minimum(zdim - 1 - z, 1))
+    to_partner(0)
+    compute(1)
     for i in range(held):
         arrived(swap.at[i], swap_recv.at[i])
-        total[i] = parts_ref[(far + core) * held + i] + swap[i]
+        total[i] = parts_ref[held + i] + swap[i]
         copy(total.at[i], cross.at[i], cross_recv.at[i], beside)
+    compute(2)
+    to_partner(2)
+    compute(3)
     base = bins * held + chan * nbins * held
     for i in range(held):
         arrived(swap.at[held + i], swap_recv.at[held + i])
         arrived(cross.at[i], cross_recv.at[i])
-        out_ref[base + i] = (
-            parts_ref[(near + core) * held + i] + swap[held + i]
-        ) + cross[i]
+        out_ref[base + i] = (parts_ref[3 * held + i] + swap[held + i]) + cross[i]
 
     events = []
     for color, (_, _, order) in enumerate(COLORS):
@@ -390,21 +396,26 @@
         run(cond, made.wait_send)
 
 
-def exchange(parts):
+def exchange(effects, nominal, observed, variance, theta, groups, counts):
     nbins, nchan = lax.axis_size("bins"), lax.axis_size("chan")
-    chans, rows, width = parts.shape
+    chans, size, channel_width = effects.shape
+    rows, width = 2 * GW + EXTRA, GW
     held = chans // nbins
-    whole = pl.BlockSpec(memory_space=pltpu.VMEM)
+    vmem = pl.BlockSpec(memory_space=pltpu.VMEM)
+    smem = pl.BlockSpec(memory_space=pltpu.SMEM)
     chips = nchan * nbins // 2
     return pl.pallas_call(
         functools.partial(exchange_kernel, 2),
-        in_specs=[whole],
-        out_specs=whole,
+        in_specs=[smem, smem, pl.BlockSpec(memory_space=pltpu.HBM), vmem, vmem, vmem, vmem],
+        out_specs=vmem,
         out_shape=jax.ShapeDtypeStruct((nchan * chans, rows, width), jnp.float32),
         scratch_shapes=[
+            pltpu.VMEM((chans, size, channel_width), jnp.bfloat16),
+            pltpu.VMEM((chans, rows, width), jnp.float32),
             pltpu.VMEM((2 * held, rows, width), jnp.float32),
             pltpu.VMEM((held, rows, width), jnp.float32),
             pltpu.VMEM((held, rows, width), jnp.float32),
+            pltpu.SemaphoreType.DMA((chans,)),
             pltpu.SemaphoreType.DMA((2 * held,)),
             pltpu.SemaphoreType.DMA((held,)),
             pltpu.SemaphoreType.DMA((len(COLORS), chips)),
@@ -415,7 +426,7 @@
             collective_id=0, has_side_effects=True, vmem_limit_bytes=32 * 2**20
         ),
         name="exchange",
-    )(parts)
+    )(groups, counts, pltpu.with_memory_space_constraint(effects, pltpu.HBM), nominal, observed, variance, theta.reshape(-1, 1, GW))
 
 
 SENDS = 240
@@ -427,12 +438,12 @@
     total_nu = theta.shape[0]
     slice_len = total_nu // devices
     groups = nuisance_index[:, ::GW] // GW
-    parts = curvature(effects, nominal, observed, mc_variance, theta, groups, bin_counts)
+    arrays = (effects, nominal, observed, mc_variance, theta, groups, bin_counts)
     chan_size, bins_size = lax.axis_size("chan"), lax.axis_size("bins")
     if bins_size == 4 and chan_size % 2 == 0 and chan_size // 2 <= DEEP:
-        payload = exchange(parts)
+        payload = exchange(*arrays)
     else:
-        summed = lax.psum_scatter(parts, "bins", scatter_dimension=0, tiled=True)
+        summed = lax.psum_scatter(curvature(*arrays), "bins", scatter_dimension=0, tiled=True)
         payload = lax.all_gather(summed, ("chan", "bins"), axis=0, tiled=True)
     tiles, grad = place(
         payload, theta, groups, tile_owner, tile_owner.shape[0] // devices, max(1, slice_len // GW)

time: 84.3 us -> 73.5 us (0.87)
  Pallas kernels: 79.5 us -> 66.6 us
  local copies, waits for them, and re-layouts: 2.17 us -> 4.85 us
    pallas_call x2 -> x1, Pallas kernels: 65.8 us -> 57.5 us  [exchange(): pl.pallas_call(functools.partial(exchange_kernel, 2), in_specs=[smem, sme...]
    pallas_call x1, Pallas kernels: 13.7 us -> 9.17 us  [place(): pl.pallas_call(place_kernel, grid_spec=pltpu.PrefetchScalarGridSpec(num_s...]
    unnamed x8 -> x12, local copies, waits for them, and re-layouts: 1.25 us -> 3.93 us
where the time goes in v3:
time: 73.5 us; the launch traced here: 72.2 us
  Pallas kernels  66.6 us (91%)
  local copies, waits for them, and re-layouts  4.85 us (7%)
    pallas_call x1, Pallas kernels, exchange(): pl.pallas_call(functools.partial(exchange_kernel, 2), in_specs=[smem, sme...  57.5 us
    pallas_call x1, Pallas kernels, place(): pl.pallas_call(place_kernel, grid_spec=pltpu.PrefetchScalarGridSpec(num_s...  9.17 us
    unnamed x12, local copies, waits for them, and re-layouts  3.93 us

profile of v3, /device:TPU:0, one launch (start us, length us, event | category | flops | bytes accessed | tf_op | source)
XLA Modules:
  0.0 72.2 jit_solution(2335474623953375753)
XLA Ops:
  0.6 0.9 %slice.3 = s32[64,2]{1,0:T(8,128)S(1)} slice(s32[64,256]{1,0:T(8,128)} %param.13), slice={[0:64:1], [0:256:128]} | slice | bytes 1024 | tf_op jit(solution)/shard_map/slice | solution.py:440
  1.6 0.0 copy-start
  1.6 0.7 %copy-done = f32[8192]{0:T(1024)S(1)} copy-done((f32[8192]{0:T(1024)S(1)}, f32[8192]{0:T(1024)}, u32[]{:S(2)}) %copy-start) | copy-done | bytes 32792
  2.3 0.0 copy-start.1
  2.3 0.8 %copy-done.1 = f32[8,2048]{1,0:T(8,128)S(1)} copy-done((f32[8,2048]{1,0:T(8,128)S(1)}, f32[8,2048]{1,0:T(8,128)}, u32[]{:S(2)}) %copy-start.1) | copy-done | bytes 65560
  3.2 0.0 copy-start.2
  3.2 0.8 %copy-done.2 = s32[8,2048]{1,0:T(8,128)S(1)} copy-done((s32[8,2048]{1,0:T(8,128)S(1)}, s32[8,2048]{1,0:T(8,128)}, u32[]{:S(2)}) %copy-start.2) | copy-done | bytes 65560
  4.0 0.0 copy-start.3
  4.0 0.8 %copy-done.3 = f32[8,2048]{1,0:T(8,128)S(1)} copy-done((f32[8,2048]{1,0:T(8,128)S(1)}, f32[8,2048]{1,0:T(8,128)}, u32[]{:S(2)}) %copy-start.3) | copy-done | bytes 65560
  4.9 0.0 copy-start.5
  4.9 0.7 copy-done.5
  5.5 0.0 copy-start.4
  5.5 57.5 %exchange.1.payload_ref = f32[64,264,128]{2,1,0:T(8,128)S(1)} custom-call(s32[64,2]{1,0:T(8,128)S(1)} %add_select_fusion.groups_ref, s32[8]{0:T(128)S(1)} %copy-done.5, bf16[8,2048,256]{2,1,0:T(8,128)(2,1)} %eff_ref.1, f32[8,2048]{1,0:T(8,128)S(1)} %copy-done.1, s32[8,2048]{1,0:T(8,128)S(1)} %copy-done.2, f32[8,2048]{1,0:T(8,128)S(1)} %copy-done.3, ...), custom_call_target="tpu_custom_call" | custom-call | tf_op jit(solution)/shard_map/exchange/pallas_call | solution.py:407
  63.0 0.0 copy-done.4
  63.0 9.2 %place.1 = (f32[8,512,512]{2,1,0:T(8,128)}, f32[2,1,128]{2,1,0:T(1,128)}) custom-call(s32[64,2]{1,0:T(8,128)S(1)} %add_select_fusion.groups_ref, s32[256]{0:T(256)S(1)} %copy-done.4, f32[64,264,128]{2,1,0:T(8,128)S(1)} %exchange.1.payload_ref, f32[64,1,128]{2,1,0:T(1,128)S(1)} %bitcast.3), custom_call_target="tpu_custom_call" | custom-call | tf_op jit(solution)/shard_map/place/pallas_call | solution.py:207
  (1 shorter events, 0.0 us)
Async XLA Ops:
  1.6 0.8 %copy-start = (f32[8192]{0:T(1024)S(1)}, f32[8192]{0:T(1024)}, u32[]{:S(2)}) copy-start(f32[8192]{0:T(1024)} %param.12) | copy-start | bytes 98308
  2.3 0.8 %copy-start.1 = (f32[8,2048]{1,0:T(8,128)S(1)}, f32[8,2048]{1,0:T(8,128)}, u32[]{:S(2)}) copy-start(f32[8,2048]{1,0:T(8,128)} %nom_ref.1) | copy-start | bytes 196612
  3.2 0.8 %copy-start.2 = (s32[8,2048]{1,0:T(8,128)S(1)}, s32[8,2048]{1,0:T(8,128)}, u32[]{:S(2)}) copy-start(s32[8,2048]{1,0:T(8,128)} %obs_ref.1) | copy-start | bytes 196612
  4.0 0.8 %copy-start.3 = (f32[8,2048]{1,0:T(8,128)S(1)}, f32[8,2048]{1,0:T(8,128)}, u32[]{:S(2)}) copy-start(f32[8,2048]{1,0:T(8,128)} %var_ref.1) | copy-start | bytes 196612
  4.9 0.7 copy-start.5
  5.5 57.5 %copy-start.4 = (s32[256]{0:T(256)S(1)}, s32[256]{0:T(256)}, u32[]{:S(2)}) copy-start(s32[256]{0:T(256)} %owner_ref.1) | copy-start | bytes 3076
